TPU v7x, 512 devices: a whole 4x4x16 slice. The times are simulated.
512 devices in a mesh: leaf: 16 (over z), row: 8 (over x, core), top: 4 (over y).
Axes of the slice: x: 4, y: 4, z: 16, core: 2. Of those that a mesh axis runs over, the one named last changes fastest.
Arguments:
- loads: bfloat16 [16, 8, 4, 1, 256, 32], P('leaf', 'row', 'top'), may hold values from -6 to 6
- flux_maps: bfloat16 [16, 8, 4, 640, 256], P('leaf', 'row', 'top'), may hold values from -0.375 to 0.375
- chain_maps: float32 [16, 8, 4, 640, 640], P('leaf', 'row', 'top')
- leaf_maps: bfloat16 [16, 8, 4, 1, 256, 256], P('leaf', 'row', 'top'), may hold values from -0.375 to 0.375
- edge_maps: bfloat16 [16, 8, 4, 1, 256, 640], P('leaf', 'row', 'top'), may hold values from -0.25 to 0.25
- top_maps: bfloat16 [16, 8, 4, 1, 256, 128], P('leaf', 'row', 'top'), may hold values from -0.5 to 0.5
- slot_nodes: int32 [16, 8, 4, 128], P('leaf', 'row', 'top'), may hold values from 0 to 8191
- slot_counts: int32 [16, 8, 4], P('leaf', 'row', 'top'), may hold values from 1 to 128, 320 in all within a row
- top_loads: float32 [8192, 32], P('leaf'), may hold values from -6 to 6
- top_inverse: float32 [8192, 8192], P('top', ('leaf', 'row')), may hold values from -0.0234375 to 0.0234375
Outputs:
- solution: bfloat16 [16, 8, 4, 1, 256, 32], P('leaf', 'row', 'top')
- top_values: float32 [8192, 32], P('top')
Inputs may be any that keep to these rules, and one draw needn't show every extreme that they name: `slot_counts`: over the 4 subtrees of one x-y cell (same x and y, all t) the live slots sum to 320, and one of those subtrees has all 128 slots live.
All inputs are finite; a program needn't handle non-finite values. No bound on the sum of `slot_counts` on one device may be relied on, other than what follows from the above.
Results may differ from a plain program's by a relative error of at most 0.0046.
Values sent between devices are 32-bit elements; how exact they have to be, the bound alone decides.
No kernel may reach another device: no remote copies, remote signals or barrier semaphores. Data moves between devices by JAX's collectives and lax.ppermute only.
A program may use at most 64 MiB of HBM per device.

v0:
```python
import jax
import jax.numpy as jnp
from jax import lax
from jax.sharding import Mesh
from jax.sharding import PartitionSpec as P

ROW_TOP = ("row_0", "row_1", "top")
ROW = ("row_0", "row_1")
LEAF_ROW = ("leaf", "row_0", "row_1")


def passed_along(value, axis, steps):
    count = lax.axis_size(axis)
    first, last = (max(0, -steps), min(count, count - steps))
    return lax.ppermute(value, axis, [(source, source + steps) for source in range(first, last)])


def split_up(value, dim, count):
    before, after = (value.shape[:dim], value.shape[dim + 1 :])
    return jnp.moveaxis(value.reshape(*before, count, -1, *after), dim, 0)


def sent_and_summed(value, axis, dim):
    pieces = split_up(value, dim, lax.axis_size(axis))
    arrived = lax.all_to_all(pieces, axis, split_axis=0, concat_axis=0, tiled=True)
    return arrived.sum(axis=0)


def rows_for(lines, count):
    spare = -lines.shape[0] % count
    if not spare:
        return lines
    return jnp.concatenate([lines, jnp.zeros((spare, *lines.shape[1:]), lines.dtype)])


def joined_along(pieces, dim):
    dims = list(pieces.shape[1:])
    dims[dim] *= pieces.shape[0]
    return jnp.moveaxis(pieces, 0, dim).reshape(dims)


def copy_for_each(value, axis):
    copies = jnp.broadcast_to(value, (lax.axis_size(axis), *value.shape))
    return lax.all_to_all(copies, axis, split_axis=0, concat_axis=0, tiled=True)


def collect(value, axis, dim):
    return joined_along(copy_for_each(value, axis), dim)


def total_of(value, axes):
    lines = value.reshape(-1, value.shape[-1])
    padded = rows_for(lines, lax.axis_size(axes))
    whole = collect(sent_and_summed(padded, axes, 0), axes, 0)
    return lax.slice_in_dim(whole, 0, len(lines)).reshape(value.shape)


def whole_of(value, axes, dim):
    far, near = axes
    first = copy_for_each(value, far)
    pieces = jnp.swapaxes(copy_for_each(first, near), 0, 1)
    return joined_along(pieces.reshape(-1, *value.shape), dim)


def summed_rows(value, axes, dim):
    far, near = axes
    pieces = split_up(value, dim, lax.axis_size(far))
    nearer = sent_and_summed(pieces, near, dim + 1)
    arrived = lax.all_to_all(nearer, far, split_axis=0, concat_axis=0, tiled=True)
    return arrived.sum(axis=0)


def nested_sum(value, axes):
    lines = value.reshape(-1, value.shape[-1])
    padded = rows_for(lines, lax.axis_size(axes[0]) * lax.axis_size(axes[1]))
    whole = whole_of(summed_rows(padded, axes, 0), axes, 0)
    return lax.slice_in_dim(whole, 0, len(lines)).reshape(value.shape)


def body(
    loads,
    flux_maps,
    chain_maps,
    leaf_maps,
    edge_maps,
    top_maps,
    slot_nodes,
    slot_counts,
    top_loads,
    top_inverse,
):
    leaf_count = loads.shape[3]
    node_count = loads.shape[4]
    rhs_count = loads.shape[5]
    sep_width = chain_maps.shape[-1]
    slot_total = slot_nodes.shape[-1]
    largest_level = lax.Precision.HIGHEST
    local_loads = loads.reshape(leaf_count, node_count, rhs_count)
    flattened = loads.reshape(leaf_count * node_count, rhs_count)
    fluxes = jnp.dot(
        flux_maps.reshape(sep_width, leaf_count * node_count),
        flattened,
        preferred_element_type=jnp.float32,
    )
    combine_operator = chain_maps.reshape(sep_width, sep_width)
    chain_index = lax.axis_index("leaf")

    def advance(step_index, carried):
        earlier = passed_along(carried, "leaf", 1)
        advanced = (
            jnp.dot(
                combine_operator,
                earlier,
                precision=largest_level,
                preferred_element_type=jnp.float32,
            )
            + fluxes
        )
        return jnp.where(chain_index == step_index, advanced, carried)

    states = lax.fori_loop(1, lax.axis_size("leaf"), advance, fluxes)
    slot_ids = slot_nodes.reshape(slot_total)
    is_live = lax.iota(jnp.int32, slot_total) < slot_counts.reshape(())
    chosen_entries = jnp.where(is_live[:, None], states[:slot_total], jnp.float32(0.0))
    block_rows = top_loads.shape[0]
    row_ids = lax.iota(jnp.int32, block_rows * lax.axis_size("leaf"))
    match_table = (row_ids[:, None] == slot_ids[None, :]).astype(jnp.float32)
    top_block = sent_and_summed(
        jnp.dot(
            match_table, chosen_entries, precision=largest_level, preferred_element_type=jnp.float32
        ),
        "leaf",
        0,
    )
    top_block = total_of(top_block, ROW_TOP)
    rhs_block = top_loads - top_block
    column_rows = top_inverse.shape[1]
    rhs_piece = lax.dynamic_slice_in_dim(
        rhs_block, lax.axis_index(ROW) * column_rows, column_rows, 0
    )
    partial_value = jnp.dot(
        top_inverse, rhs_piece, precision=largest_level, preferred_element_type=jnp.float32
    )
    owned_rows = nested_sum(partial_value, (("leaf", "row_0"), "row_1"))
    shard_piece = collect(owned_rows, "top", 0)
    row_ids = lax.iota(jnp.int32, shard_piece.shape[0])
    match_table = ((slot_ids[:, None] == row_ids[None, :]) & is_live[:, None]).astype(jnp.float32)
    boundary = jnp.dot(
        match_table, shard_piece, precision=largest_level, preferred_element_type=jnp.float32
    )
    states_low = states.astype(jnp.bfloat16)
    boundary_low = boundary.astype(jnp.bfloat16)
    summed = jnp.einsum(
        "lij,ljr->lir",
        leaf_maps.reshape(leaf_count, node_count, node_count),
        local_loads,
        preferred_element_type=jnp.float32,
    )
    summed = summed + jnp.einsum(
        "lik,kr->lir",
        edge_maps.reshape(leaf_count, node_count, sep_width),
        states_low,
        preferred_element_type=jnp.float32,
    )
    summed = summed + jnp.einsum(
        "lic,cr->lir",
        top_maps.reshape(leaf_count, node_count, slot_total),
        boundary_low,
        preferred_element_type=jnp.float32,
    )
    solution = summed.astype(jnp.bfloat16).reshape(1, 1, 1, leaf_count, node_count, rhs_count)
    return (solution, owned_rows)


def solution(mesh):
    split = Mesh(
        mesh.devices.reshape(mesh.shape["leaf"], 4, 2, mesh.shape["top"]),
        ("leaf", "row_0", "row_1", "top"),
    )
    placed = (
        P("leaf", ROW, "top", None, None, None),
        P("leaf", ROW, "top", None, None),
        P("leaf", ROW, "top", None, None),
        P("leaf", ROW, "top", None, None, None),
        P("leaf", ROW, "top", None, None, None),
        P("leaf", ROW, "top", None, None, None),
        P("leaf", ROW, "top", None),
        P("leaf", ROW, "top"),
        P("leaf", None),
        P("top", LEAF_ROW),
    )
    return jax.shard_map(
        body,
        mesh=split,
        in_specs=placed,
        out_specs=(P("leaf", ROW, "top", None, None, None), P("top", None)),
        check_vma=False,
    )
```

profile of v0, /device:TPU:1, one launch (start us, length us, event | category | flops | bytes accessed | tf_op | source)
XLA Modules:
  0.0 333.8 jit_solution(12857406827622153484)
XLA Ops:
  2.6 139.4 %while.13 = (s32[]{:T(128)}, f32[640,32]{0,1:T(8,128)S(1)}, s32[]{:T(128)}, f32[640,640]{1,0:T(8,128)}, f32[640,32]{0,1:T(8,128)S(1)}, /*index=5*/s32[]{:T(128)}) while((s32[]{:T(128)}, f32[640,32]{0,1:T(8,128)S(1)}, s32[]{:T(128)}, f32[640,640]{1,0:T(8,128)}, f32[640,32]{0,1:T(8,128)S(1)}, /*index=5*/s32[]{:T(128)}) %tuple.40), condition=%wide.region_1.2_spmd, body=%wide.region_0.1_spmd.sunk | while | flops 157327360 | bytes 2293879 | solution.py:121
  2.6 4.4 %collective-permute-start = (f32[640,32]{0,1:T(8,128)S(1)}, f32[640,32]{0,1:T(8,128)S(1)}, u32[]{:S(2)}, u32[]{:S(2)}) collective-permute-start(f32[640,32]{0,1:T(8,128)S(1)} %get-tuple-element.155), channel_id=1, source_target_pairs={{0,32},{32,64},{64,96},{96,128},{128,160},{160,192},{192,224},{224... | collective-permute-start | bytes 245768 | tf_op jit(solution)/shard_map/while/body/eval_jaxpr/ppermute | solution.py:15
  8.4 3.1 fusion.38
  11.5 3.7 %collective-permute-start = (f32[640,32]{0,1:T(8,128)S(1)}, f32[640,32]{0,1:T(8,128)S(1)}, u32[]{:S(2)}, u32[]{:S(2)}) collective-permute-start(f32[640,32]{0,1:T(8,128)S(1)} %get-tuple-element.155), channel_id=1, source_target_pairs={{0,32},{32,64},{64,96},{96,128},{128,160},{160,192},{192,224},{224... | collective-permute-start | bytes 245768 | tf_op jit(solution)/shard_map/while/body/eval_jaxpr/ppermute | solution.py:15
  16.7 3.1 fusion.38
  19.8 3.7 %collective-permute-start = (f32[640,32]{0,1:T(8,128)S(1)}, f32[640,32]{0,1:T(8,128)S(1)}, u32[]{:S(2)}, u32[]{:S(2)}) collective-permute-start(f32[640,32]{0,1:T(8,128)S(1)} %get-tuple-element.155), channel_id=1, source_target_pairs={{0,32},{32,64},{64,96},{96,128},{128,160},{160,192},{192,224},{224... | collective-permute-start | bytes 245768 | tf_op jit(solution)/shard_map/while/body/eval_jaxpr/ppermute | solution.py:15
  24.9 3.1 fusion.38
  28.0 4.4 %collective-permute-start = (f32[640,32]{0,1:T(8,128)S(1)}, f32[640,32]{0,1:T(8,128)S(1)}, u32[]{:S(2)}, u32[]{:S(2)}) collective-permute-start(f32[640,32]{0,1:T(8,128)S(1)} %get-tuple-element.155), channel_id=1, source_target_pairs={{0,32},{32,64},{64,96},{96,128},{128,160},{160,192},{192,224},{224... | collective-permute-start | bytes 245768 | tf_op jit(solution)/shard_map/while/body/eval_jaxpr/ppermute | solution.py:15
  33.9 3.1 fusion.38
  37.0 4.9 %collective-permute-start = (f32[640,32]{0,1:T(8,128)S(1)}, f32[640,32]{0,1:T(8,128)S(1)}, u32[]{:S(2)}, u32[]{:S(2)}) collective-permute-start(f32[640,32]{0,1:T(8,128)S(1)} %get-tuple-element.155), channel_id=1, source_target_pairs={{0,32},{32,64},{64,96},{96,128},{128,160},{160,192},{192,224},{224... | collective-permute-start | bytes 245768 | tf_op jit(solution)/shard_map/while/body/eval_jaxpr/ppermute | solution.py:15
  46.5 4.9 %collective-permute-start = (f32[640,32]{0,1:T(8,128)S(1)}, f32[640,32]{0,1:T(8,128)S(1)}, u32[]{:S(2)}, u32[]{:S(2)}) collective-permute-start(f32[640,32]{0,1:T(8,128)S(1)} %get-tuple-element.155), channel_id=1, source_target_pairs={{0,32},{32,64},{64,96},{96,128},{128,160},{160,192},{192,224},{224... | collective-permute-start | bytes 245768 | tf_op jit(solution)/shard_map/while/body/eval_jaxpr/ppermute | solution.py:15
  55.9 4.9 %collective-permute-start = (f32[640,32]{0,1:T(8,128)S(1)}, f32[640,32]{0,1:T(8,128)S(1)}, u32[]{:S(2)}, u32[]{:S(2)}) collective-permute-start(f32[640,32]{0,1:T(8,128)S(1)} %get-tuple-element.155), channel_id=1, source_target_pairs={{0,32},{32,64},{64,96},{96,128},{128,160},{160,192},{192,224},{224... | collective-permute-start | bytes 245768 | tf_op jit(solution)/shard_map/while/body/eval_jaxpr/ppermute | solution.py:15
  65.4 4.9 %collective-permute-start = (f32[640,32]{0,1:T(8,128)S(1)}, f32[640,32]{0,1:T(8,128)S(1)}, u32[]{:S(2)}, u32[]{:S(2)}) collective-permute-start(f32[640,32]{0,1:T(8,128)S(1)} %get-tuple-element.155), channel_id=1, source_target_pairs={{0,32},{32,64},{64,96},{96,128},{128,160},{160,192},{192,224},{224... | collective-permute-start | bytes 245768 | tf_op jit(solution)/shard_map/while/body/eval_jaxpr/ppermute | solution.py:15
  74.8 4.9 %collective-permute-start = (f32[640,32]{0,1:T(8,128)S(1)}, f32[640,32]{0,1:T(8,128)S(1)}, u32[]{:S(2)}, u32[]{:S(2)}) collective-permute-start(f32[640,32]{0,1:T(8,128)S(1)} %get-tuple-element.155), channel_id=1, source_target_pairs={{0,32},{32,64},{64,96},{96,128},{128,160},{160,192},{192,224},{224... | collective-permute-start | bytes 245768 | tf_op jit(solution)/shard_map/while/body/eval_jaxpr/ppermute | solution.py:15
  84.3 4.9 %collective-permute-start = (f32[640,32]{0,1:T(8,128)S(1)}, f32[640,32]{0,1:T(8,128)S(1)}, u32[]{:S(2)}, u32[]{:S(2)}) collective-permute-start(f32[640,32]{0,1:T(8,128)S(1)} %get-tuple-element.155), channel_id=1, source_target_pairs={{0,32},{32,64},{64,96},{96,128},{128,160},{160,192},{192,224},{224... | collective-permute-start | bytes 245768 | tf_op jit(solution)/shard_map/while/body/eval_jaxpr/ppermute | solution.py:15
  91.5 3.1 fusion.38
  94.6 4.8 %collective-permute-start = (f32[640,32]{0,1:T(8,128)S(1)}, f32[640,32]{0,1:T(8,128)S(1)}, u32[]{:S(2)}, u32[]{:S(2)}) collective-permute-start(f32[640,32]{0,1:T(8,128)S(1)} %get-tuple-element.155), channel_id=1, source_target_pairs={{0,32},{32,64},{64,96},{96,128},{128,160},{160,192},{192,224},{224... | collective-permute-start | bytes 245768 | tf_op jit(solution)/shard_map/while/body/eval_jaxpr/ppermute | solution.py:15
  103.9 4.9 %collective-permute-start = (f32[640,32]{0,1:T(8,128)S(1)}, f32[640,32]{0,1:T(8,128)S(1)}, u32[]{:S(2)}, u32[]{:S(2)}) collective-permute-start(f32[640,32]{0,1:T(8,128)S(1)} %get-tuple-element.155), channel_id=1, source_target_pairs={{0,32},{32,64},{64,96},{96,128},{128,160},{160,192},{192,224},{224... | collective-permute-start | bytes 245768 | tf_op jit(solution)/shard_map/while/body/eval_jaxpr/ppermute | solution.py:15
  113.4 4.8 %collective-permute-start = (f32[640,32]{0,1:T(8,128)S(1)}, f32[640,32]{0,1:T(8,128)S(1)}, u32[]{:S(2)}, u32[]{:S(2)}) collective-permute-start(f32[640,32]{0,1:T(8,128)S(1)} %get-tuple-element.155), channel_id=1, source_target_pairs={{0,32},{32,64},{64,96},{96,128},{128,160},{160,192},{192,224},{224... | collective-permute-start | bytes 245768 | tf_op jit(solution)/shard_map/while/body/eval_jaxpr/ppermute | solution.py:15
  122.8 5.2 %collective-permute-start = (f32[640,32]{0,1:T(8,128)S(1)}, f32[640,32]{0,1:T(8,128)S(1)}, u32[]{:S(2)}, u32[]{:S(2)}) collective-permute-start(f32[640,32]{0,1:T(8,128)S(1)} %get-tuple-element.155), channel_id=1, source_target_pairs={{0,32},{32,64},{64,96},{96,128},{128,160},{160,192},{192,224},{224... | collective-permute-start | bytes 245768 | tf_op jit(solution)/shard_map/while/body/eval_jaxpr/ppermute | solution.py:15
  132.6 4.9 %collective-permute-start = (f32[640,32]{0,1:T(8,128)S(1)}, f32[640,32]{0,1:T(8,128)S(1)}, u32[]{:S(2)}, u32[]{:S(2)}) collective-permute-start(f32[640,32]{0,1:T(8,128)S(1)} %get-tuple-element.155), channel_id=1, source_target_pairs={{0,32},{32,64},{64,96},{96,128},{128,160},{160,192},{192,224},{224... | collective-permute-start | bytes 245768 | tf_op jit(solution)/shard_map/while/body/eval_jaxpr/ppermute | solution.py:15
  144.4 49.8 %all_to_all.40 = f32[16,512,32]{1,2,0:T(8,128)S(1)} all-to-all(f32[16,512,32]{1,2,0:T(8,128)S(1)} %bitcast.69), channel_id=1, replica_groups=mesh['leaf'=16,'row_0'=4,'row_1'=2,'top'=4] {'leaf'}, dimensions={0} | all-to-all | bytes 2097152 | tf_op jit(solution)/shard_map/all_to_all | solution.py:25
  195.2 27.8 %all-to-all-start.1 = ((f32[32,1,512]{2,1,0:T(1,128)}), f32[32,1,512]{2,1,0:T(1,128)S(1)}, u32[]{:S(2)}, u32[]{:S(2)}) async-start(f32[32,1,512]{2,1,0:T(1,128)} %reshape.74), calls=%async_computation.1 | async-start | bytes 131072 | tf_op jit(solution)/shard_map/all_to_all | solution.py:25
  223.1 7.3 %all-to-all-done.1 = f32[32,1,512]{2,1,0:T(1,128)S(1)} async-done(((f32[32,1,512]{2,1,0:T(1,128)}), f32[32,1,512]{2,1,0:T(1,128)S(1)}, u32[]{:S(2)}, u32[]{:S(2)}) %all-to-all-start.1) | async-done | bytes 65568 | tf_op jit(solution)/shard_map/all_to_all | solution.py:25
  232.6 3.9 %all-to-all-start.2 = ((f32[32,1,512]{2,1,0:T(1,128)}), f32[32,1,512]{2,1,0:T(1,128)S(1)}, u32[]{:S(2)}, u32[]{:S(2)}) async-start(f32[32,1,512]{2,1,0:T(1,128)} %reshape.76), calls=%async_computation.2 | async-start | bytes 131072 | tf_op jit(solution)/shard_map/all_to_all | solution.py:44
  237.4 6.5 %all-to-all-done.2 = f32[32,1,512]{2,1,0:T(1,128)S(1)} async-done(((f32[32,1,512]{2,1,0:T(1,128)}), f32[32,1,512]{2,1,0:T(1,128)S(1)}, u32[]{:S(2)}, u32[]{:S(2)}) %all-to-all-start.2) | async-done | bytes 65568 | tf_op jit(solution)/shard_map/all_to_all | solution.py:44
  246.6 4.0 %all_to_all.41 = f32[2,1,32768]{2,1,0:T(1,128)S(1)} all-to-all(f32[2,1,32768]{2,1,0:T(1,128)S(1)} %reshape.78), channel_id=1, replica_groups=mesh['leaf'=16,'row_0'=4,'row_1'=2,'top'=4] {'row_1'}, dimensions={0} | all-to-all | bytes 524288 | tf_op jit(solution)/shard_map/all_to_all | solution.py:25
  252.9 23.6 %all_to_all.42 = f32[64,1,512]{2,1,0:T(1,128)S(1)} all-to-all(f32[64,1,512]{2,1,0:T(1,128)S(1)} %reshape.80), channel_id=1, replica_groups=mesh['leaf'=16,'row_0'=4,'row_1'=2,'top'=4] {'leaf','row_0'}, dimensions={0} | all-to-all | bytes 262144 | tf_op jit(solution)/shard_map/all_to_all | solution.py:69
  278.1 21.3 %all_to_all.43 = f32[64,1,512]{2,1,0:T(1,128)S(1)} all-to-all(f32[64,1,512]{2,1,0:T(1,128)S(1)} %reshape.82), channel_id=1, replica_groups=mesh['leaf'=16,'row_0'=4,'row_1'=2,'top'=4] {'leaf','row_0'}, dimensions={0} | all-to-all | bytes 262144 | tf_op jit(solution)/shard_map/all_to_all | solution.py:44
  301.1 6.8 %all_to_all.44 = f32[2,1,32768]{2,1,0:T(1,128)S(1)} all-to-all(f32[2,1,32768]{2,1,0:T(1,128)S(1)} %reshape.84), channel_id=1, replica_groups=mesh['leaf'=16,'row_0'=4,'row_1'=2,'top'=4] {'row_1'}, dimensions={0} | all-to-all | bytes 524288 | tf_op jit(solution)/shard_map/all_to_all | solution.py:44
  312.1 3.5 %all-to-all-start.7 = ((f32[4,2048,32]{1,2,0:T(8,128)}), f32[4,2048,32]{1,2,0:T(8,128)S(1)}, u32[]{:S(2)}, u32[]{:S(2)}) async-start(f32[4,2048,32]{1,2,0:T(8,128)} %broadcast_in_dim.33), calls=%async_computation.7 | async-start | bytes 2097152 | tf_op jit(solution)/shard_map/all_to_all | solution.py:44
  316.0 14.4 %all-to-all-done.7 = f32[4,2048,32]{1,2,0:T(8,128)S(1)} async-done(((f32[4,2048,32]{1,2,0:T(8,128)}), f32[4,2048,32]{1,2,0:T(8,128)S(1)}, u32[]{:S(2)}, u32[]{:S(2)}) %all-to-all-start.7) | async-done | bytes 1048608 | tf_op jit(solution)/shard_map/all_to_all | solution.py:44
  (87 shorter events, 77.0 us)
Async XLA Ops:
  0.6 244.2 %copy-start = (f32[2048,64]{0,1:T(8,128)S(1)}, f32[2048,64]{0,1:T(8,128)}, u32[]{:S(2)}) copy-start(f32[2048,64]{0,1:T(8,128)} %param.21) | copy-start | bytes 1572868
  2.6 139.5 %copy-start.6 = (s32[1,1,1,128]{3,2,1,0:T(1,128)S(1)}, s32[1,1,1,128]{3,2,1,0:T(1,128)}, u32[]{:S(2)}) copy-start(s32[1,1,1,128]{3,2,1,0:T(1,128)} %param.18) | copy-start | bytes 1540
  2.6 5.8 %collective-permute-start = (f32[640,32]{0,1:T(8,128)S(1)}, f32[640,32]{0,1:T(8,128)S(1)}, u32[]{:S(2)}, u32[]{:S(2)}) collective-permute-start(f32[640,32]{0,1:T(8,128)S(1)} %get-tuple-element.155), channel_id=1, source_target_pairs={{0,32},{32,64},{64,96},{96,128},{128,160},{160,192},{192,224},{224... | collective-permute-start | bytes 245768 | tf_op jit(solution)/shard_map/while/body/eval_jaxpr/ppermute | solution.py:15
  11.5 5.2 %collective-permute-start = (f32[640,32]{0,1:T(8,128)S(1)}, f32[640,32]{0,1:T(8,128)S(1)}, u32[]{:S(2)}, u32[]{:S(2)}) collective-permute-start(f32[640,32]{0,1:T(8,128)S(1)} %get-tuple-element.155), channel_id=1, source_target_pairs={{0,32},{32,64},{64,96},{96,128},{128,160},{160,192},{192,224},{224... | collective-permute-start | bytes 245768 | tf_op jit(solution)/shard_map/while/body/eval_jaxpr/ppermute | solution.py:15
  19.8 5.2 %collective-permute-start = (f32[640,32]{0,1:T(8,128)S(1)}, f32[640,32]{0,1:T(8,128)S(1)}, u32[]{:S(2)}, u32[]{:S(2)}) collective-permute-start(f32[640,32]{0,1:T(8,128)S(1)} %get-tuple-element.155), channel_id=1, source_target_pairs={{0,32},{32,64},{64,96},{96,128},{128,160},{160,192},{192,224},{224... | collective-permute-start | bytes 245768 | tf_op jit(solution)/shard_map/while/body/eval_jaxpr/ppermute | solution.py:15
  28.0 5.9 %collective-permute-start = (f32[640,32]{0,1:T(8,128)S(1)}, f32[640,32]{0,1:T(8,128)S(1)}, u32[]{:S(2)}, u32[]{:S(2)}) collective-permute-start(f32[640,32]{0,1:T(8,128)S(1)} %get-tuple-element.155), channel_id=1, source_target_pairs={{0,32},{32,64},{64,96},{96,128},{128,160},{160,192},{192,224},{224... | collective-permute-start | bytes 245768 | tf_op jit(solution)/shard_map/while/body/eval_jaxpr/ppermute | solution.py:15
  37.0 6.4 %collective-permute-start = (f32[640,32]{0,1:T(8,128)S(1)}, f32[640,32]{0,1:T(8,128)S(1)}, u32[]{:S(2)}, u32[]{:S(2)}) collective-permute-start(f32[640,32]{0,1:T(8,128)S(1)} %get-tuple-element.155), channel_id=1, source_target_pairs={{0,32},{32,64},{64,96},{96,128},{128,160},{160,192},{192,224},{224... | collective-permute-start | bytes 245768 | tf_op jit(solution)/shard_map/while/body/eval_jaxpr/ppermute | solution.py:15
  46.5 6.4 %collective-permute-start = (f32[640,32]{0,1:T(8,128)S(1)}, f32[640,32]{0,1:T(8,128)S(1)}, u32[]{:S(2)}, u32[]{:S(2)}) collective-permute-start(f32[640,32]{0,1:T(8,128)S(1)} %get-tuple-element.155), channel_id=1, source_target_pairs={{0,32},{32,64},{64,96},{96,128},{128,160},{160,192},{192,224},{224... | collective-permute-start | bytes 245768 | tf_op jit(solution)/shard_map/while/body/eval_jaxpr/ppermute | solution.py:15
  55.9 6.4 %collective-permute-start = (f32[640,32]{0,1:T(8,128)S(1)}, f32[640,32]{0,1:T(8,128)S(1)}, u32[]{:S(2)}, u32[]{:S(2)}) collective-permute-start(f32[640,32]{0,1:T(8,128)S(1)} %get-tuple-element.155), channel_id=1, source_target_pairs={{0,32},{32,64},{64,96},{96,128},{128,160},{160,192},{192,224},{224... | collective-permute-start | bytes 245768 | tf_op jit(solution)/shard_map/while/body/eval_jaxpr/ppermute | solution.py:15
  65.4 6.4 %collective-permute-start = (f32[640,32]{0,1:T(8,128)S(1)}, f32[640,32]{0,1:T(8,128)S(1)}, u32[]{:S(2)}, u32[]{:S(2)}) collective-permute-start(f32[640,32]{0,1:T(8,128)S(1)} %get-tuple-element.155), channel_id=1, source_target_pairs={{0,32},{32,64},{64,96},{96,128},{128,160},{160,192},{192,224},{224... | collective-permute-start | bytes 245768 | tf_op jit(solution)/shard_map/while/body/eval_jaxpr/ppermute | solution.py:15
  74.8 6.4 %collective-permute-start = (f32[640,32]{0,1:T(8,128)S(1)}, f32[640,32]{0,1:T(8,128)S(1)}, u32[]{:S(2)}, u32[]{:S(2)}) collective-permute-start(f32[640,32]{0,1:T(8,128)S(1)} %get-tuple-element.155), channel_id=1, source_target_pairs={{0,32},{32,64},{64,96},{96,128},{128,160},{160,192},{192,224},{224... | collective-permute-start | bytes 245768 | tf_op jit(solution)/shard_map/while/body/eval_jaxpr/ppermute | solution.py:15
  84.3 7.2 %collective-permute-start = (f32[640,32]{0,1:T(8,128)S(1)}, f32[640,32]{0,1:T(8,128)S(1)}, u32[]{:S(2)}, u32[]{:S(2)}) collective-permute-start(f32[640,32]{0,1:T(8,128)S(1)} %get-tuple-element.155), channel_id=1, source_target_pairs={{0,32},{32,64},{64,96},{96,128},{128,160},{160,192},{192,224},{224... | collective-permute-start | bytes 245768 | tf_op jit(solution)/shard_map/while/body/eval_jaxpr/ppermute | solution.py:15
  94.6 6.3 %collective-permute-start = (f32[640,32]{0,1:T(8,128)S(1)}, f32[640,32]{0,1:T(8,128)S(1)}, u32[]{:S(2)}, u32[]{:S(2)}) collective-permute-start(f32[640,32]{0,1:T(8,128)S(1)} %get-tuple-element.155), channel_id=1, source_target_pairs={{0,32},{32,64},{64,96},{96,128},{128,160},{160,192},{192,224},{224... | collective-permute-start | bytes 245768 | tf_op jit(solution)/shard_map/while/body/eval_jaxpr/ppermute | solution.py:15
  103.9 6.4 %collective-permute-start = (f32[640,32]{0,1:T(8,128)S(1)}, f32[640,32]{0,1:T(8,128)S(1)}, u32[]{:S(2)}, u32[]{:S(2)}) collective-permute-start(f32[640,32]{0,1:T(8,128)S(1)} %get-tuple-element.155), channel_id=1, source_target_pairs={{0,32},{32,64},{64,96},{96,128},{128,160},{160,192},{192,224},{224... | collective-permute-start | bytes 245768 | tf_op jit(solution)/shard_map/while/body/eval_jaxpr/ppermute | solution.py:15
  113.4 6.3 %collective-permute-start = (f32[640,32]{0,1:T(8,128)S(1)}, f32[640,32]{0,1:T(8,128)S(1)}, u32[]{:S(2)}, u32[]{:S(2)}) collective-permute-start(f32[640,32]{0,1:T(8,128)S(1)} %get-tuple-element.155), channel_id=1, source_target_pairs={{0,32},{32,64},{64,96},{96,128},{128,160},{160,192},{192,224},{224... | collective-permute-start | bytes 245768 | tf_op jit(solution)/shard_map/while/body/eval_jaxpr/ppermute | solution.py:15
  122.8 6.7 %collective-permute-start = (f32[640,32]{0,1:T(8,128)S(1)}, f32[640,32]{0,1:T(8,128)S(1)}, u32[]{:S(2)}, u32[]{:S(2)}) collective-permute-start(f32[640,32]{0,1:T(8,128)S(1)} %get-tuple-element.155), channel_id=1, source_target_pairs={{0,32},{32,64},{64,96},{96,128},{128,160},{160,192},{192,224},{224... | collective-permute-start | bytes 245768 | tf_op jit(solution)/shard_map/while/body/eval_jaxpr/ppermute | solution.py:15
  132.6 6.4 %collective-permute-start = (f32[640,32]{0,1:T(8,128)S(1)}, f32[640,32]{0,1:T(8,128)S(1)}, u32[]{:S(2)}, u32[]{:S(2)}) collective-permute-start(f32[640,32]{0,1:T(8,128)S(1)} %get-tuple-element.155), channel_id=1, source_target_pairs={{0,32},{32,64},{64,96},{96,128},{128,160},{160,192},{192,224},{224... | collective-permute-start | bytes 245768 | tf_op jit(solution)/shard_map/while/body/eval_jaxpr/ppermute | solution.py:15
  195.2 35.1 %all-to-all-start.1 = ((f32[32,1,512]{2,1,0:T(1,128)}), f32[32,1,512]{2,1,0:T(1,128)S(1)}, u32[]{:S(2)}, u32[]{:S(2)}) async-start(f32[32,1,512]{2,1,0:T(1,128)} %reshape.74), calls=%async_computation.1 | async-start | bytes 131072 | tf_op jit(solution)/shard_map/all_to_all | solution.py:25
  232.6 11.3 %all-to-all-start.2 = ((f32[32,1,512]{2,1,0:T(1,128)}), f32[32,1,512]{2,1,0:T(1,128)S(1)}, u32[]{:S(2)}, u32[]{:S(2)}) async-start(f32[32,1,512]{2,1,0:T(1,128)} %reshape.76), calls=%async_computation.2 | async-start | bytes 131072 | tf_op jit(solution)/shard_map/all_to_all | solution.py:44
  311.0 1.1 copy-start.1
  311.0 4.7 %copy-start.2 = (bf16[1,1,1,1,256,640]{5,4,3,2,1,0:T(8,128)(2,1)S(1)}, bf16[1,1,1,1,256,640]{5,4,3,2,1,0:T(8,128)(2,1)}, u32[]{:S(2)}) copy-start(bf16[1,1,1,1,256,640]{5,4,3,2,1,0:T(8,128)(2,1)} %param.16) | copy-start | bytes 983044
  311.0 4.8 %copy-start.3 = (bf16[1,1,1,1,256,256]{5,4,3,2,1,0:T(8,128)(2,1)S(1)}, bf16[1,1,1,1,256,256]{5,4,3,2,1,0:T(8,128)(2,1)}, u32[]{:S(2)}) copy-start(bf16[1,1,1,1,256,256]{5,4,3,2,1,0:T(8,128)(2,1)} %param.15) | copy-start | bytes 393220
  311.0 4.8 %copy-start.5 = (bf16[1,1,1,1,256,32]{4,5,3,2,1,0:T(8,128)(2,1)S(1)}, bf16[1,1,1,1,256,32]{4,5,3,2,1,0:T(8,128)(2,1)}, u32[]{:S(2)}) copy-start(bf16[1,1,1,1,256,32]{4,5,3,2,1,0:T(8,128)(2,1)} %param.12) | copy-start | bytes 49156
  312.1 18.3 %all-to-all-start.7 = ((f32[4,2048,32]{1,2,0:T(8,128)}), f32[4,2048,32]{1,2,0:T(8,128)S(1)}, u32[]{:S(2)}, u32[]{:S(2)}) async-start(f32[4,2048,32]{1,2,0:T(8,128)} %broadcast_in_dim.33), calls=%async_computation.7 | async-start | bytes 2097152 | tf_op jit(solution)/shard_map/all_to_all | solution.py:44
  330.5 2.5 copy-start.4
where the time goes:
time: 335 us; the launch traced here: 334 us
  starting transfers between devices  106 us (32%)
  blocking collectives  105 us (31%)
  matrix products  53.3 us (16%)
  waiting for transfers between devices  50.8 us (15%)
  local copies, waits for them, and re-layouts  9.72 us (3%)
  other arithmetic  6.63 us (2%)
    ppermute x15, starting transfers between devices, passed_along(): lax.ppermute(value, axis, [(source, source + steps) for source in range(f...  70.5 us
    all_to_all x2, blocking collectives, sent_and_summed(): lax.all_to_all(pieces, axis, split_axis=0, concat_axis=0, tiled=True)  53.7 us
    dot_general x15, matrix products, advance(): jnp.dot(combine_operator, earlier, precision=largest_level, preferred_ele...  45.8 us
    all_to_all x2, blocking collectives, copy_for_each(): return lax.all_to_all(copies, axis, split_axis=0, concat_axis=0, tiled=True)  28.1 us
    all_to_all x1, starting transfers between devices, sent_and_summed(): lax.all_to_all(pieces, axis, split_axis=0, concat_axis=0, tiled=True)  27.8 us
    all_to_all x1, blocking collectives, summed_rows(): lax.all_to_all(nearer, far, split_axis=0, concat_axis=0, tiled=True)  23.6 us
    ppermute x15, waiting for transfers between devices, passed_along(): lax.ppermute(value, axis, [(source, source + steps) for source in range(f...  22.6 us
    all_to_all x2, waiting for transfers between devices, copy_for_each(): return lax.all_to_all(copies, axis, split_axis=0, concat_axis=0, tiled=True)  20.9 us
  transfers between devices with their start and end apart: 18, of which 18 were waited for; matrix products, arithmetic and copies ran while one was open for 0% of the time, Pallas kernels for 0%

commit v1 on v0

v1 whole, which is shorter than its diff:
```python
import jax
import jax.numpy as jnp
from jax import lax
from jax.sharding import Mesh
from jax.sharding import PartitionSpec as P


ROW = ("row_0", "row_1")
ROW_TOP = ("row_0", "row_1", "top")
LEAF_ROW = ("leaf", "row_0", "row_1")


def exchanged(pieces, axes):
    return lax.all_to_all(pieces, axes, split_axis=0, concat_axis=0, tiled=True)


def copies_from_all(value, axes):
    return exchanged(jnp.broadcast_to(value, (lax.axis_size(axes), *value.shape)), axes)


def parts_of(value):
    high = lax.reduce_precision(value, 8, 7)
    return high.astype(jnp.bfloat16), (value - high).astype(jnp.bfloat16)


def stacked_parts(value, dim):
    return jnp.concatenate(parts_of(value), dim)


def contract_last(left, right):
    return lax.dot_general(
        left, right, (((1,), (1,)), ((), ())), preferred_element_type=jnp.float32
    )


def mapped(stacked_map, state, flux):
    count, width = state.shape
    product = contract_last(stacked_parts(state, 0), stacked_map)
    return product[:count, :width] + product[count:, :width] + product[:count, width:] + flux


def chain(chain_map, flux):
    planes = lax.axis_size("leaf")
    plane = lax.axis_index("leaf")
    half = planes // 2

    def sent(value, pairs):
        return lax.ppermute(value, "leaf", pairs)

    pairs = [(even, even + 1) for even in range(half, planes, 2)]
    map_before = sent(chain_map, pairs)
    flux_before = sent(flux, pairs)
    own = lax.optimization_barrier(stacked_parts(chain_map, 0))
    state = flux
    for step in range(1, half):
        arrived = sent(state, [(step - 1, step)])
        state = jnp.where(plane == step, mapped(own, arrived, flux), state)
    previous = stacked_parts(map_before, 0)
    for step in range(half + 1, planes, 2):
        arrived = sent(state, [(step - 2, step)])
        advanced = mapped(own, mapped(previous, arrived, flux_before), flux)
        state = jnp.where(plane == step, advanced, state)
    beside = sent(state, [(even - 1, even) for even in range(half, planes, 2)])
    is_even = (plane >= half) & (plane % 2 == 0)
    return jnp.where(is_even, mapped(own, beside, flux), state)


def body(
    loads,
    flux_maps,
    chain_maps,
    leaf_maps,
    edge_maps,
    top_maps,
    slot_nodes,
    slot_counts,
    top_loads,
    top_inverse,
):
    nodes, rhs = loads.shape[4:]
    width = chain_maps.shape[-1]
    slots = slot_nodes.shape[-1]
    leaf_size = lax.axis_size("leaf")
    row_size = lax.axis_size(ROW)
    top_size = lax.axis_size("top")
    block = top_loads.shape[0]
    share, columns = top_inverse.shape
    local_loads = loads.reshape(nodes, rhs)

    flux = lax.dot_general(
        local_loads,
        flux_maps.reshape(width, nodes),
        (((0,), (1,)), ((), ())),
        preferred_element_type=jnp.float32,
    )
    states = chain(chain_maps.reshape(width, width), flux)

    live = lax.iota(jnp.int32, slots) < slot_counts.reshape(())
    ids = jnp.where(live, slot_nodes.reshape(slots), -1)
    id_row = ids.astype(jnp.float32)[None]
    entries = copies_from_all(jnp.concatenate([states[:, :slots], id_row]), "leaf")

    first_node = lax.axis_index("leaf") * block
    entry_ids = entries[:, rhs].astype(jnp.int32).reshape(1, -1) - first_node
    match = (lax.iota(jnp.int32, block)[:, None] == entry_ids).astype(jnp.bfloat16)
    values = jnp.swapaxes(entries[:, :rhs], 0, 1).reshape(rhs, -1)
    dense = contract_last(stacked_parts(values, 0), match)
    dense = (dense[:rhs] + dense[rhs:]).reshape(2, rhs // 2, row_size, columns)
    packed = dense.transpose(2, 1, 0, 3).reshape(row_size, 1, rhs // 2, 2 * columns)
    packed = jnp.broadcast_to(packed, (row_size, top_size, rhs // 2, 2 * columns))
    own_ids = jnp.broadcast_to(id_row, (row_size, top_size, 1, slots))
    pieces = jnp.concatenate([packed, own_ids], 2)
    arrived = exchanged(pieces.reshape(-1, *pieces.shape[2:]), ROW_TOP)

    row = lax.axis_index(ROW)
    top_sum = arrived[:, : rhs // 2].sum(0).reshape(rhs // 2, 2, columns)
    top_sum = top_sum.transpose(1, 0, 2).reshape(rhs, columns)
    cell_ids = lax.dynamic_slice_in_dim(arrived[:, rhs // 2], row * top_size, top_size, 0)
    own_top_loads = lax.dynamic_slice_in_dim(top_loads, row * columns, columns, 0)
    top_rhs = own_top_loads.T - top_sum
    high, low = parts_of(top_rhs)
    inverse = stacked_parts(top_inverse, 1)
    left = jnp.concatenate(
        [jnp.concatenate([high, high], 1), jnp.concatenate([low, jnp.zeros_like(low)], 1)]
    )
    partial = contract_last(left, inverse)
    partial = partial[:rhs] + partial[rhs:]

    group = rhs // row_size
    by_row = exchanged(partial.reshape(row_size, group, share), ROW).sum(0)
    lanes = share // leaf_size
    by_leaf = jnp.swapaxes(by_row.reshape(group, leaf_size, lanes), 0, 1)
    finished = exchanged(by_leaf, "leaf").sum(0)
    band = jnp.swapaxes(copies_from_all(finished, "leaf"), 0, 1).reshape(group, share)
    values = copies_from_all(band, ROW).reshape(rhs, share)

    first_value = lax.axis_index("top") * share
    wanted = cell_ids.astype(jnp.int32).reshape(1, -1) - first_value
    match = (lax.iota(jnp.int32, share)[:, None] == wanted).astype(jnp.bfloat16)
    chosen = jnp.dot(values.astype(jnp.bfloat16), match, preferred_element_type=jnp.float32)
    chosen = jnp.swapaxes(chosen.reshape(rhs, top_size, slots), 0, 1)
    boundary = exchanged(chosen, "top").sum(0)

    summed = jnp.dot(
        leaf_maps.reshape(nodes, nodes), local_loads, preferred_element_type=jnp.float32
    )
    summed = summed + contract_last(
        edge_maps.reshape(nodes, width), states.astype(jnp.bfloat16)
    )
    summed = summed + contract_last(
        top_maps.reshape(nodes, slots), boundary.astype(jnp.bfloat16)
    )
    solution = summed.astype(jnp.bfloat16).reshape(1, 1, 1, 1, nodes, rhs)
    return solution, values.T


def solution(mesh):
    split = Mesh(
        mesh.devices.reshape(mesh.shape["leaf"], -1, 2, mesh.shape["top"]),
        ("leaf", "row_0", "row_1", "top"),
    )
    placed = (
        P("leaf", ROW, "top", None, None, None),
        P("leaf", ROW, "top", None, None),
        P("leaf", ROW, "top", None, None),
        P("leaf", ROW, "top", None, None, None),
        P("leaf", ROW, "top", None, None, None),
        P("leaf", ROW, "top", None, None, None),
        P("leaf", ROW, "top", None),
        P("leaf", ROW, "top"),
        P("leaf", None),
        P("top", LEAF_ROW),
    )

    return jax.shard_map(
        body,
        mesh=split,
        in_specs=placed,
        out_specs=(P("leaf", ROW, "top", None, None, None), P("top", None)),
        check_vma=False,
    )
```

time: 335 us -> 204 us (0.61)
  blocking collectives: 105 us -> 9.54 us
  matrix products: 53.3 us -> 17.6 us
  local copies, waits for them, and re-layouts: 9.72 us -> 4.8 us
  waiting for transfers between devices: 50.8 us -> 55.4 us
    all_to_all x5 -> x1, blocking collectives: 105 us -> 9.54 us  [exchanged(): return lax.all_to_all(pieces, axes, split_axis=0, concat_axis=0, tiled=True)]
    all_to_all x3 -> x6, starting transfers between devices: 35.3 us -> 91.7 us  [exchanged(): return lax.all_to_all(pieces, axes, split_axis=0, concat_axis=0, tiled=True)]
    ppermute x15 -> x14, starting transfers between devices: 70.5 us -> 14.2 us  [sent(): return lax.ppermute(value, 'leaf', pairs)]
    dot_general x22 -> x23, matrix products: 53.3 us -> 17.6 us  [the longest x20 15.2 us: contract_last(): lax.dot_general(left, right, (((1,), (1,)), ((), ())), preferred_element_...]
    all_to_all x3 -> x6, waiting for transfers between devices: 28.1 us -> 55.3 us  [exchanged(): return lax.all_to_all(pieces, axes, split_axis=0, concat_axis=0, tiled=True)]
    ppermute x15 -> x14, waiting for transfers between devices: 22.6 us -> 0.04 us  [sent(): return lax.ppermute(value, 'leaf', pairs)]
    all_to_all x6 -> x0, other arithmetic: 6.38 us -> none  [the longest x3 3.19 us: copy_for_each(): return lax.all_to_all(copies, axis, split_axis=0, concat_axis=0, tiled=True)]
    convert_element_type x0 -> x28, other arithmetic: none -> 4.6 us  [the longest x25 4.54 us: parts_of(): return (high.astype(jnp.bfloat16), (value - high).astype(jnp.bfloat16))]
  transfers between devices with their start and end apart: 18 -> 20, of which waited for: 18 -> 6; matrix products, arithmetic and copies ran while one was open for 0% -> 4% of each run, Pallas kernels for 0% -> 0%
where the time goes in v1:
time: 204 us; the launch traced here: 203 us
  starting transfers between devices  106 us (52%)
  waiting for transfers between devices  55.4 us (27%)
  matrix products  17.6 us (9%)
  blocking collectives  9.54 us (5%)
  other arithmetic  7.31 us (4%)
  local copies, waits for them, and re-layouts  4.8 us (2%)
  between operations  2.12 us (1%)
    all_to_all x6, starting transfers between devices, exchanged(): return lax.all_to_all(pieces, axes, split_axis=0, concat_axis=0, tiled=True)  91.7 us
    all_to_all x6, waiting for transfers between devices, exchanged(): return lax.all_to_all(pieces, axes, split_axis=0, concat_axis=0, tiled=True)  55.3 us
    dot_general x20, matrix products, contract_last(): lax.dot_general(left, right, (((1,), (1,)), ((), ())), preferred_element_...  15.2 us
    ppermute x14, starting transfers between devices, sent(): return lax.ppermute(value, 'leaf', pairs)  14.2 us
    all_to_all x1, blocking collectives, exchanged(): return lax.all_to_all(pieces, axes, split_axis=0, concat_axis=0, tiled=True)  9.54 us
    convert_element_type x25, other arithmetic, parts_of(): return (high.astype(jnp.bfloat16), (value - high).astype(jnp.bfloat16))  4.54 us
  transfers between devices with their start and end apart: 20, of which 6 were waited for; matrix products, arithmetic and copies ran while one was open for 4% of the time, Pallas kernels for 0%

profile of v1, /device:TPU:1, one launch (start us, length us, event | category | flops | bytes accessed | tf_op | source)
XLA Modules:
  0.0 202.6 jit_solution(9929568138671295639)
XLA Ops:
  0.6 1.0 copy-done
  1.6 0.9 fusion.13
  2.5 4.4 %collective-permute-start = (f32[32,640]{1,0:T(8,128)S(1)}, f32[32,640]{1,0:T(8,128)S(1)}, u32[]{:S(2)}, u32[]{:S(2)}) collective-permute-start(f32[32,640]{1,0:T(8,128)S(1)} %fusion.13), channel_id=1, source_target_pairs={{0,32},{1,33},{2,34},{3,35},{4,36},{5,37},{6,38},{7,39},{8,40},{9,... | collective-permute-start | bytes 245768 | tf_op jit(solution)/shard_map/ppermute | solution.py:48
  6.9 1.7 reduce-precision_convert_fusion.1
  9.4 0.7 collective-permute-start.1
  10.8 0.7 collective-permute-start.2
  15.5 1.9 collective-permute-start.8
  20.8 1.7 reduce-precision_convert_fusion
  24.7 1.7 fusion.98
  27.9 1.7 fusion.106
  31.7 1.8 fusion.114
  35.5 0.8 broadcast_in_dim.30
  36.3 56.7 %all-to-all-start = ((f32[16,33,128]{2,1,0:T(8,128)}), f32[16,33,128]{2,1,0:T(8,128)S(1)}, u32[]{:S(2)}, u32[]{:S(2)}) async-start(f32[16,33,128]{2,1,0:T(8,128)} %broadcast_in_dim.30), calls=%async_computation | async-start | bytes 655360 | tf_op jit(solution)/shard_map/all_to_all | solution.py:14
  93.0 13.5 %all-to-all-done = f32[16,33,128]{2,1,0:T(8,128)S(1)} async-done(((f32[16,33,128]{2,1,0:T(8,128)}), f32[16,33,128]{2,1,0:T(8,128)S(1)}, u32[]{:S(2)}, u32[]{:S(2)}) %all-to-all-start) | async-done | bytes 270368 | tf_op jit(solution)/shard_map/all_to_all | solution.py:14
  106.6 0.9 fusion
  107.9 0.8 pad_maximum_fusion.2
  108.6 17.7 %all-to-all-start.1 = ((f32[32,17,128]{2,1,0:T(8,128)}), f32[32,17,128]{2,1,0:T(8,128)S(1)}, u32[]{:S(2)}, u32[]{:S(2)}) async-start(f32[32,17,128]{2,1,0:T(8,128)} %bitcast.13), calls=%async_computation.1 | async-start | bytes 786432 | tf_op jit(solution)/shard_map/all_to_all | solution.py:14
  126.5 10.0 %all-to-all-done.1 = f32[32,17,128]{2,1,0:T(8,128)S(1)} async-done(((f32[32,17,128]{2,1,0:T(8,128)}), f32[32,17,128]{2,1,0:T(8,128)S(1)}, u32[]{:S(2)}, u32[]{:S(2)}) %all-to-all-start.1) | async-done | bytes 278560 | tf_op jit(solution)/shard_map/all_to_all | solution.py:14
  136.6 0.8 reduce-precision_convert_fusion.20
  137.8 9.5 %all_to_all.35 = f32[8,4,2048]{2,1,0:T(4,128)S(1)} all-to-all(f32[8,4,2048]{2,1,0:T(4,128)S(1)} %reshape.149), channel_id=1, replica_groups=mesh['leaf'=16,'row_0'=4,'row_1'=2,'top'=4] {'row_0','row_1'}, dimensions={0} | all-to-all | bytes 524288 | tf_op jit(solution)/shard_map/all_to_all | solution.py:14
  148.0 3.5 %all-to-all-start.3 = ((f32[16,4,128]{2,1,0:T(4,128)}), f32[16,4,128]{2,1,0:T(4,128)S(1)}, u32[]{:S(2)}, u32[]{:S(2)}) async-start(f32[16,4,128]{2,1,0:T(4,128)} %bitcast.17), calls=%async_computation.3 | async-start | bytes 65536 | tf_op jit(solution)/shard_map/all_to_all | solution.py:14
  151.5 11.5 %all-to-all-done.3 = f32[16,4,128]{2,1,0:T(4,128)S(1)} async-done(((f32[16,4,128]{2,1,0:T(4,128)}), f32[16,4,128]{2,1,0:T(4,128)S(1)}, u32[]{:S(2)}, u32[]{:S(2)}) %all-to-all-start.3) | async-done | bytes 32800 | tf_op jit(solution)/shard_map/all_to_all | solution.py:14
  163.7 3.5 %all-to-all-start.4 = ((f32[16,4,128]{2,1,0:T(4,128)}), f32[16,4,128]{2,1,0:T(4,128)S(1)}, u32[]{:S(2)}, u32[]{:S(2)}) async-start(f32[16,4,128]{2,1,0:T(4,128)} %broadcast_in_dim.35), calls=%async_computation.4 | async-start | bytes 65536 | tf_op jit(solution)/shard_map/all_to_all | solution.py:14
  167.4 11.1 %all-to-all-done.4 = f32[16,4,128]{2,1,0:T(4,128)S(1)} async-done(((f32[16,4,128]{2,1,0:T(4,128)}), f32[16,4,128]{2,1,0:T(4,128)S(1)}, u32[]{:S(2)}, u32[]{:S(2)}) %all-to-all-start.4) | async-done | bytes 32800 | tf_op jit(solution)/shard_map/all_to_all | solution.py:14
  178.5 0.7 broadcast_in_dim.36
  179.3 6.9 %all-to-all-start.5 = ((f32[8,4,2048]{2,1,0:T(4,128)}), f32[8,4,2048]{2,1,0:T(4,128)S(1)}, u32[]{:S(2)}, u32[]{:S(2)}) async-start(f32[8,4,2048]{2,1,0:T(4,128)} %broadcast_in_dim.36), calls=%async_computation.5 | async-start | bytes 524288 | tf_op jit(solution)/shard_map/all_to_all | solution.py:14
  186.9 5.8 %all-to-all-done.5 = f32[8,4,2048]{2,1,0:T(4,128)S(1)} async-done(((f32[8,4,2048]{2,1,0:T(4,128)}), f32[8,4,2048]{2,1,0:T(4,128)S(1)}, u32[]{:S(2)}, u32[]{:S(2)}) %all-to-all-start.5) | async-done | bytes 262176 | tf_op jit(solution)/shard_map/all_to_all | solution.py:14
  192.8 1.3 convolution_bitcast_fusion
  194.1 3.3 %all-to-all-start.6 = ((f32[4,32,128]{2,1,0:T(8,128)}), f32[4,32,128]{2,1,0:T(8,128)S(1)}, u32[]{:S(2)}, u32[]{:S(2)}) async-start(f32[4,32,128]{2,1,0:T(8,128)} %convolution_bitcast_fusion), calls=%async_computation.6 | async-start | bytes 131072 | tf_op jit(solution)/shard_map/all_to_all | solution.py:14
  197.6 0.8 reshape.154
  198.4 3.4 %all-to-all-done.6 = f32[4,32,128]{2,1,0:T(8,128)S(1)} async-done(((f32[4,32,128]{2,1,0:T(8,128)}), f32[4,32,128]{2,1,0:T(8,128)S(1)}, u32[]{:S(2)}, u32[]{:S(2)}) %all-to-all-start.6) | async-done | bytes 65568 | tf_op jit(solution)/shard_map/all_to_all | solution.py:14
  201.8 0.8 fusion.6
  (115 shorter events, 19.1 us)
Async XLA Ops:
  0.6 1.0 copy-start
  2.5 6.2 %collective-permute-start = (f32[32,640]{1,0:T(8,128)S(1)}, f32[32,640]{1,0:T(8,128)S(1)}, u32[]{:S(2)}, u32[]{:S(2)}) collective-permute-start(f32[32,640]{1,0:T(8,128)S(1)} %fusion.13), channel_id=1, source_target_pairs={{0,32},{1,33},{2,34},{3,35},{4,36},{5,37},{6,38},{7,39},{8,40},{9,... | collective-permute-start | bytes 245768 | tf_op jit(solution)/shard_map/ppermute | solution.py:48
  9.4 0.7 collective-permute-start.1
  10.8 0.7 collective-permute-start.2
  12.1 0.7 collective-permute-start.3
  13.5 0.7 collective-permute-start.4
  14.8 2.5 %collective-permute-start.5 = (f32[32,640]{1,0:T(8,128)S(1)}, f32[32,640]{1,0:T(8,128)S(1)}, u32[]{:S(2)}, u32[]{:S(2)}) collective-permute-start(f32[32,640]{1,0:T(8,128)S(1)} %fusion.55), channel_id=1, source_target_pairs={{160,192},{161,193},{162,194},{163,195},{164,196},{165,197},{166,1... | collective-permute-start | bytes 245768 | tf_op jit(solution)/shard_map/ppermute | solution.py:48
  15.5 5.3 %collective-permute-start.8 = (f32[640,640]{1,0:T(8,128)}, f32[640,640]{1,0:T(8,128)}, u32[]{:S(2)}, u32[]{:S(2)}) collective-permute-start(f32[640,640]{1,0:T(8,128)} %bitcast.3), channel_id=1, source_target_pairs={{256,288},{320,352},{384,416},{448,480},{257,289},{321,353},{385,4... | collective-permute-start | bytes 4915208 | tf_op jit(solution)/shard_map/ppermute | solution.py:48
  18.0 0.7 collective-permute-start.6
  19.4 1.4 collective-permute-start.7
  20.1 3.0 %collective-permute-start.9 = (f32[32,640]{1,0:T(8,128)S(1)}, f32[32,640]{1,0:T(8,128)S(1)}, u32[]{:S(2)}, u32[]{:S(2)}) collective-permute-start(f32[32,640]{1,0:T(8,128)S(1)} %fusion.13), channel_id=1, source_target_pairs={{256,288},{320,352},{384,416},{448,480},{257,289},{321,353},{385,4... | collective-permute-start | bytes 245768 | tf_op jit(solution)/shard_map/ppermute | solution.py:48
  22.4 0.9 copy-start.1
  24.0 0.7 collective-permute-start.10
  27.1 0.7 collective-permute-start.11
  30.3 1.3 collective-permute-start.12
  33.4 1.4 copy-start.7
  34.1 0.7 collective-permute-start.13
  36.3 70.2 %all-to-all-start = ((f32[16,33,128]{2,1,0:T(8,128)}), f32[16,33,128]{2,1,0:T(8,128)S(1)}, u32[]{:S(2)}, u32[]{:S(2)}) async-start(f32[16,33,128]{2,1,0:T(8,128)} %broadcast_in_dim.30), calls=%async_computation | async-start | bytes 655360 | tf_op jit(solution)/shard_map/all_to_all | solution.py:14
  107.5 18.9 %copy-start.2 = (f32[2048,64]{0,1:T(8,128)S(1)}, f32[2048,64]{0,1:T(8,128)}, u32[]{:S(2)}) copy-start(f32[2048,64]{0,1:T(8,128)} %param.19) | copy-start | bytes 1572868
  108.6 27.8 %all-to-all-start.1 = ((f32[32,17,128]{2,1,0:T(8,128)}), f32[32,17,128]{2,1,0:T(8,128)S(1)}, u32[]{:S(2)}, u32[]{:S(2)}) async-start(f32[32,17,128]{2,1,0:T(8,128)} %bitcast.13), calls=%async_computation.1 | async-start | bytes 786432 | tf_op jit(solution)/shard_map/all_to_all | solution.py:14
  137.4 29.8 %copy-start.3 = (bf16[1,1,1,1,256,640]{5,4,3,2,1,0:T(8,128)(2,1)S(1)}, bf16[1,1,1,1,256,640]{5,4,3,2,1,0:T(8,128)(2,1)}, u32[]{:S(2)}) copy-start(bf16[1,1,1,1,256,640]{5,4,3,2,1,0:T(8,128)(2,1)} %param.14) | copy-start | bytes 983044
  148.0 15.0 %all-to-all-start.3 = ((f32[16,4,128]{2,1,0:T(4,128)}), f32[16,4,128]{2,1,0:T(4,128)S(1)}, u32[]{:S(2)}, u32[]{:S(2)}) async-start(f32[16,4,128]{2,1,0:T(4,128)} %bitcast.17), calls=%async_computation.3 | async-start | bytes 65536 | tf_op jit(solution)/shard_map/all_to_all | solution.py:14
  163.7 14.9 %all-to-all-start.4 = ((f32[16,4,128]{2,1,0:T(4,128)}), f32[16,4,128]{2,1,0:T(4,128)S(1)}, u32[]{:S(2)}, u32[]{:S(2)}) async-start(f32[16,4,128]{2,1,0:T(4,128)} %broadcast_in_dim.35), calls=%async_computation.4 | async-start | bytes 65536 | tf_op jit(solution)/shard_map/all_to_all | solution.py:14
  179.3 13.4 %all-to-all-start.5 = ((f32[8,4,2048]{2,1,0:T(4,128)}), f32[8,4,2048]{2,1,0:T(4,128)S(1)}, u32[]{:S(2)}, u32[]{:S(2)}) async-start(f32[8,4,2048]{2,1,0:T(4,128)} %broadcast_in_dim.36), calls=%async_computation.5 | async-start | bytes 524288 | tf_op jit(solution)/shard_map/all_to_all | solution.py:14
  186.2 11.2 %copy-start.4 = (bf16[1,1,1,1,256,256]{5,4,3,2,1,0:T(8,128)(2,1)S(1)}, bf16[1,1,1,1,256,256]{5,4,3,2,1,0:T(8,128)(2,1)}, u32[]{:S(2)}) copy-start(bf16[1,1,1,1,256,256]{5,4,3,2,1,0:T(8,128)(2,1)} %param.13) | copy-start | bytes 393220
  186.2 11.2 %copy-start.6 = (bf16[1,1,1,1,256,32]{4,5,3,2,1,0:T(8,128)(2,1)S(1)}, bf16[1,1,1,1,256,32]{4,5,3,2,1,0:T(8,128)(2,1)}, u32[]{:S(2)}) copy-start(bf16[1,1,1,1,256,32]{4,5,3,2,1,0:T(8,128)(2,1)} %param.10) | copy-start | bytes 49156
  186.8 15.0 %copy-start.5 = (bf16[1,1,1,1,256,128]{5,4,3,2,1,0:T(8,128)(2,1)S(1)}, bf16[1,1,1,1,256,128]{5,4,3,2,1,0:T(8,128)(2,1)}, u32[]{:S(2)}) copy-start(bf16[1,1,1,1,256,128]{5,4,3,2,1,0:T(8,128)(2,1)} %param.15) | copy-start | bytes 196612
  194.1 7.7 %all-to-all-start.6 = ((f32[4,32,128]{2,1,0:T(8,128)}), f32[4,32,128]{2,1,0:T(8,128)S(1)}, u32[]{:S(2)}, u32[]{:S(2)}) async-start(f32[4,32,128]{2,1,0:T(8,128)} %convolution_bitcast_fusion), calls=%async_computation.6 | async-start | bytes 131072 | tf_op jit(solution)/shard_map/all_to_all | solution.py:14
